TPU v7x, 32 devices: a whole 2x2x4 slice. The times are simulated.
32 devices in a mesh: fsdp: 4 (over x, core), ctx: 8 (over z, y).
Axes of the slice: x: 2, y: 2, z: 4, core: 2. Of those that a mesh axis runs over, the one named last changes fastest.
Arguments:
- inputs: bfloat16 [4096, 1536], P(('fsdp', 'ctx')), may hold values from -6 to 6
- positions: int32 [4096], P(('fsdp', 'ctx')), may hold values from 0 to 1023, as said below
- cotangent: bfloat16 [4096, 1536], P(('fsdp', 'ctx')), may hold values from -6 to 6
- attention_gain: bfloat16 [1536], replicated, may hold values from 0.5 to 1.5
- query_weight: bfloat16 [1536, 1536], P('fsdp'), may hold values from -0.15625 to 0.15625
- key_weight: bfloat16 [768, 1536], P('fsdp'), may hold values from -0.15625 to 0.15625
- value_weight: bfloat16 [768, 1536], P('fsdp'), may hold values from -0.15625 to 0.15625
- output_weight: bfloat16 [1536, 1536], P('fsdp'), may hold values from -3 to 3
- feedforward_gain: bfloat16 [1536], replicated, may hold values from 0.5 to 1.5
- gate_weight: bfloat16 [4096, 1536], P('fsdp'), may hold values from -0.15625 to 0.15625
- up_weight: bfloat16 [4096, 1536], P('fsdp'), may hold values from -0.15625 to 0.15625
- down_weight: bfloat16 [4096, 1536], P('fsdp'), may hold values from -0.09375 to 0.09375
Outputs:
- layer_output: bfloat16 [4096, 1536], P(('fsdp', 'ctx'))
- input_grad: float32 [4096, 1536], P(('fsdp', 'ctx'))
- attention_gain_grad: float32 [1536], replicated
- query_weight_grad: float32 [1536, 1536], P('fsdp')
- key_weight_grad: float32 [768, 1536], P('fsdp')
- value_weight_grad: float32 [768, 1536], P('fsdp')
- output_weight_grad: float32 [1536, 1536], P('fsdp')
- feedforward_gain_grad: float32 [1536], replicated
- gate_weight_grad: float32 [4096, 1536], P('fsdp')
- up_weight_grad: float32 [4096, 1536], P('fsdp')
- down_weight_grad: float32 [4096, 1536], P('fsdp')
Inputs may be any that keep to these rules, and one draw needn't show every extreme that they name: Within each sequence every position appears once, and each device's 2 * 64 tokens of a sequence are two whole blocks of 64 consecutive rising positions, starting at b * 64 and at (15 - b) * 64 for some b, in either order.
All inputs are finite; a program needn't handle non-finite values.
Results may differ from a plain program's by a relative error of at most 0.022.
Values may be sent and summed in bfloat16 or wider, within the bound.
A program may use at most 384 MiB of HBM per device.

v0:
```python
import math
import jax
import jax.numpy as jnp
from jax import lax
from jax.sharding import PartitionSpec as P

HEADS = 16
KV_HEADS = 8
HEAD_DIM = 96
EPSILON = 1e-05
ROPE_BASE = 100000.0


def product(left, right):
    return jnp.dot(left, right, preferred_element_type=jnp.float32)


def product_back(left, right):
    return lax.dot_general(
        left, right, (((1,), (1,)), ((), ())), preferred_element_type=jnp.float32
    )


def product_rows(left, right):
    return lax.dot_general(
        left, right, (((0,), (0,)), ((), ())), preferred_element_type=jnp.float32
    )


def rms_scale(values):
    return lax.rsqrt(jnp.mean(values * values, axis=-1, keepdims=True) + EPSILON)


def norm_back(scale_rows, unit_rows, grad_unit):
    return scale_rows * (
        grad_unit - unit_rows * jnp.mean(grad_unit * unit_rows, axis=-1, keepdims=True)
    )


def rotary_tables(places):
    half_width = HEAD_DIM // 2
    frequencies = ROPE_BASE ** (-(jnp.arange(half_width, dtype=jnp.float32) * 2.0 / HEAD_DIM))
    angles = places.astype(jnp.float32)[:, None] * frequencies[None, :]
    return (jnp.cos(angles)[:, None, :], jnp.sin(angles)[:, None, :])


def rotate(values, cosine, sine):
    half_width = values.shape[-1] // 2
    lower_half = values[..., :half_width]
    upper_half = values[..., half_width:]
    return jnp.concatenate(
        [lower_half * cosine - upper_half * sine, upper_half * cosine + lower_half * sine], axis=-1
    )


def rotate_back(grads, cosine, sine):
    half_width = grads.shape[-1] // 2
    lower_half = grads[..., :half_width]
    upper_half = grads[..., half_width:]
    return jnp.concatenate(
        [lower_half * cosine + upper_half * sine, upper_half * cosine - lower_half * sine], axis=-1
    )


def block_total_of(total_keys):
    return max(1, total_keys // 512)


def masked_scores(query_grouped, query_places, key_rows, key_places, start, width):
    key_part = lax.dynamic_slice_in_dim(key_rows, start, width, 1)
    place_part = lax.dynamic_slice_in_dim(key_places, start, width, 1)
    scores = jnp.einsum(
        "sqhgd,skhd->shgqk", query_grouped, key_part, preferred_element_type=jnp.float32
    )
    scores = scores * (1.0 / math.sqrt(HEAD_DIM))
    allowed = place_part[:, None, None, None, :] <= query_places[:, None, None, :, None]
    return jnp.where(allowed, scores, -1000000000.0)


def attend_forward(query_grouped, query_places, key_rows, value_rows, key_places):
    seq_count, row_count, head_groups, group_size = query_grouped.shape[:4]
    total_keys = key_rows.shape[1]
    block_total = block_total_of(total_keys)
    width = total_keys // block_total
    stat_shape = (seq_count, head_groups, group_size, row_count)

    def peak_step(index, carry):
        running_top, running_sum = carry
        scores = masked_scores(
            query_grouped, query_places, key_rows, key_places, index * width, width
        )
        new_top = jnp.maximum(running_top, jnp.max(scores, axis=-1))
        running_sum = running_sum * jnp.exp(running_top - new_top) + jnp.sum(
            jnp.exp(scores - new_top[..., None]), axis=-1
        )
        return (new_top, running_sum)

    running_top, running_sum = lax.fori_loop(
        0,
        block_total,
        peak_step,
        (jnp.full(stat_shape, -1e30, jnp.float32), jnp.zeros(stat_shape, jnp.float32)),
    )
    log_total = running_top + jnp.log(running_sum)

    def value_step(index, gathered):
        scores = masked_scores(
            query_grouped, query_places, key_rows, key_places, index * width, width
        )
        soft_low = jnp.exp(scores - log_total[..., None]).astype(jnp.bfloat16)
        value_part = lax.dynamic_slice_in_dim(value_rows, index * width, width, 1)
        return gathered + jnp.einsum(
            "shgqk,skhd->sqhgd", soft_low, value_part, preferred_element_type=jnp.float32
        )

    attended = lax.fori_loop(
        0, block_total, value_step, jnp.zeros(query_grouped.shape, jnp.float32)
    )
    return (attended, log_total)


def attend_backward(
    query_grouped, query_places, key_rows, value_rows, key_places, log_total, grad_attended
):
    total_keys = key_rows.shape[1]
    block_total = block_total_of(total_keys)
    width = total_keys // block_total
    score_scale = 1.0 / math.sqrt(HEAD_DIM)

    def soft_and_grad(index):
        scores = masked_scores(
            query_grouped, query_places, key_rows, key_places, index * width, width
        )
        soft_values = jnp.exp(scores - log_total[..., None])
        value_part = lax.dynamic_slice_in_dim(value_rows, index * width, width, 1)
        grad_soft = jnp.einsum(
            "sqhgd,skhd->shgqk", grad_attended, value_part, preferred_element_type=jnp.float32
        )
        return (soft_values, grad_soft)

    def delta_step(index, row_delta):
        soft_values, grad_soft = soft_and_grad(index)
        return row_delta + jnp.sum(soft_values * grad_soft, axis=-1)

    row_delta = lax.fori_loop(0, block_total, delta_step, jnp.zeros(log_total.shape, jnp.float32))

    def grad_step(index, carry):
        grad_query, grad_keys, grad_values = carry
        soft_values, grad_soft = soft_and_grad(index)
        grad_scores = (soft_values * (grad_soft - row_delta[..., None])).astype(jnp.bfloat16)
        key_part = lax.dynamic_slice_in_dim(key_rows, index * width, width, 1)
        grad_query = (
            grad_query
            + jnp.einsum(
                "shgqk,skhd->sqhgd", grad_scores, key_part, preferred_element_type=jnp.float32
            )
            * score_scale
        )
        key_term = (
            jnp.einsum(
                "shgqk,sqhgd->skhd", grad_scores, query_grouped, preferred_element_type=jnp.float32
            )
            * score_scale
        )
        value_term = jnp.einsum(
            "shgqk,sqhgd->skhd",
            soft_values.astype(jnp.bfloat16),
            grad_attended,
            preferred_element_type=jnp.float32,
        )
        grad_keys = lax.dynamic_update_slice_in_dim(grad_keys, key_term, index * width, 1)
        grad_values = lax.dynamic_update_slice_in_dim(grad_values, value_term, index * width, 1)
        return (grad_query, grad_keys, grad_values)

    initial = (
        jnp.zeros(query_grouped.shape, jnp.float32),
        jnp.zeros(key_rows.shape, jnp.float32),
        jnp.zeros(value_rows.shape, jnp.float32),
    )
    return lax.fori_loop(0, block_total, grad_step, initial)


def per_device(
    inputs,
    positions,
    cotangent,
    attention_gain,
    query_weight,
    key_weight,
    value_weight,
    output_weight,
    feedforward_gain,
    gate_weight,
    up_weight,
    down_weight,
):
    row_count = inputs.shape[0]
    groups = HEADS // KV_HEADS
    gain_one = attention_gain.astype(jnp.float32)
    gain_two = feedforward_gain.astype(jnp.float32)
    seq_count = 1

    def attention_set():
        return (
            lax.all_gather(query_weight, "fsdp", axis=0, tiled=True),
            lax.all_gather(key_weight, "fsdp", axis=0, tiled=True),
            lax.all_gather(value_weight, "fsdp", axis=0, tiled=True),
            lax.all_gather(output_weight, "fsdp", axis=0, tiled=True),
        )

    def feedforward_set():
        return (
            lax.all_gather(gate_weight, "fsdp", axis=0, tiled=True),
            lax.all_gather(up_weight, "fsdp", axis=0, tiled=True),
            lax.all_gather(down_weight, "fsdp", axis=0, tiled=True),
        )

    query_places = positions.reshape(1, row_count)
    key_places = lax.all_gather(positions, "ctx", axis=0, tiled=True).reshape(1, -1)
    flat_in = inputs.astype(jnp.float32)
    scale_one = rms_scale(flat_in)
    unit_one = flat_in * scale_one
    normed_one = (unit_one * gain_one).astype(jnp.bfloat16)
    total_rows = normed_one.shape[0]
    cosine, sine = rotary_tables(query_places.reshape(-1))
    fwd_query, fwd_key, fwd_value, fwd_output = attention_set()
    query_heads = fwd_query.shape[0] // HEAD_DIM
    kv_heads = fwd_key.shape[0] // HEAD_DIM
    kv_width = kv_heads * HEAD_DIM
    query_low = rotate(
        product_back(normed_one, fwd_query).reshape(total_rows, query_heads, HEAD_DIM), cosine, sine
    ).astype(jnp.bfloat16)
    key_low = rotate(
        product_back(normed_one, fwd_key).reshape(total_rows, kv_heads, HEAD_DIM), cosine, sine
    ).astype(jnp.bfloat16)
    value_low = product_back(normed_one, fwd_value).astype(jnp.bfloat16)
    all_keys, all_values = (
        lax.all_gather(key_low.reshape(seq_count, row_count, kv_width), "ctx", axis=1, tiled=True),
        lax.all_gather(
            value_low.reshape(seq_count, row_count, kv_width), "ctx", axis=1, tiled=True
        ),
    )
    total_keys = all_keys.shape[1]
    key_grid = all_keys.reshape(seq_count, total_keys, kv_heads, HEAD_DIM)
    value_grid = all_values.reshape(seq_count, total_keys, kv_heads, HEAD_DIM)
    query_grouped = query_low.reshape(seq_count, row_count, kv_heads, groups, HEAD_DIM)
    attended, log_total = attend_forward(
        query_grouped, query_places, key_grid, value_grid, key_places
    )
    attended_low = attended.reshape(total_rows, query_heads * HEAD_DIM).astype(jnp.bfloat16)
    hidden_state = flat_in + product(attended_low, fwd_output)
    scale_two = rms_scale(hidden_state)
    unit_two = hidden_state * scale_two
    normed_two = (unit_two * gain_two).astype(jnp.bfloat16)
    fwd_gate, fwd_up, fwd_down = feedforward_set()
    gate_values = product_back(normed_two, fwd_gate)
    upward = product_back(normed_two, fwd_up)
    sigmoid_gate = jax.nn.sigmoid(gate_values)
    activated = gate_values * sigmoid_gate
    mixed_hidden = (activated * upward).astype(jnp.bfloat16)
    layer_output = (hidden_state + product(mixed_hidden, fwd_down)).astype(jnp.bfloat16)
    grad_out = cotangent.astype(jnp.float32)
    back_gate, back_up, back_down = feedforward_set()
    grad_down = product_rows(mixed_hidden, cotangent)
    grad_mixed = product_back(cotangent, back_down)
    grad_gate_low = (
        grad_mixed * upward * sigmoid_gate * (1.0 + gate_values * (1.0 - sigmoid_gate))
    ).astype(jnp.bfloat16)
    grad_up_low = (grad_mixed * activated).astype(jnp.bfloat16)
    grad_gate = product_rows(grad_gate_low, normed_two)
    grad_up = product_rows(grad_up_low, normed_two)
    feedforward_shards = (
        lax.psum_scatter(
            grad_gate.astype(jnp.bfloat16), "fsdp", scatter_dimension=0, tiled=True
        ).astype(jnp.float32),
        lax.psum_scatter(
            grad_up.astype(jnp.bfloat16), "fsdp", scatter_dimension=0, tiled=True
        ).astype(jnp.float32),
        lax.psum_scatter(
            grad_down.astype(jnp.bfloat16), "fsdp", scatter_dimension=0, tiled=True
        ).astype(jnp.float32),
    )
    grad_normed_two = product(grad_gate_low, back_gate) + product(grad_up_low, back_up)
    gain_two_grad = jnp.sum(grad_normed_two * unit_two, axis=0)
    grad_hidden = grad_out + norm_back(scale_two, unit_two, grad_normed_two * gain_two)
    branch_rows = grad_hidden.astype(jnp.bfloat16)
    back_query, back_key, back_value, back_output = attention_set()
    grad_output = product_rows(attended_low, branch_rows)
    grad_attended = product_back(branch_rows, back_output).astype(jnp.bfloat16)
    grad_attended = grad_attended.reshape(seq_count, row_count, kv_heads, groups, HEAD_DIM)
    grad_query_rot, grad_key_all, grad_value_all = attend_backward(
        query_grouped, query_places, key_grid, value_grid, key_places, log_total, grad_attended
    )
    key_grad_own, value_grad_own = (
        lax.psum_scatter(
            grad_key_all.reshape(seq_count, total_keys, kv_width).astype(jnp.bfloat16),
            "ctx",
            scatter_dimension=1,
            tiled=True,
        ).astype(jnp.float32),
        lax.psum_scatter(
            grad_value_all.reshape(seq_count, total_keys, kv_width).astype(jnp.bfloat16),
            "ctx",
            scatter_dimension=1,
            tiled=True,
        ).astype(jnp.float32),
    )
    grad_query_low = (
        rotate_back(grad_query_rot.reshape(total_rows, query_heads, HEAD_DIM), cosine, sine)
        .reshape(total_rows, query_heads * HEAD_DIM)
        .astype(jnp.bfloat16)
    )
    grad_key_low = (
        rotate_back(key_grad_own.reshape(total_rows, kv_heads, HEAD_DIM), cosine, sine)
        .reshape(total_rows, kv_width)
        .astype(jnp.bfloat16)
    )
    grad_value_low = value_grad_own.reshape(total_rows, kv_width).astype(jnp.bfloat16)
    grad_query = product_rows(grad_query_low, normed_one)
    grad_key = product_rows(grad_key_low, normed_one)
    grad_value = product_rows(grad_value_low, normed_one)
    attention_shards = (
        lax.psum_scatter(
            grad_query.astype(jnp.bfloat16), "fsdp", scatter_dimension=0, tiled=True
        ).astype(jnp.float32),
        lax.psum_scatter(
            grad_key.astype(jnp.bfloat16), "fsdp", scatter_dimension=0, tiled=True
        ).astype(jnp.float32),
        lax.psum_scatter(
            grad_value.astype(jnp.bfloat16), "fsdp", scatter_dimension=0, tiled=True
        ).astype(jnp.float32),
        lax.psum_scatter(
            grad_output.astype(jnp.bfloat16), "fsdp", scatter_dimension=0, tiled=True
        ).astype(jnp.float32),
    )
    grad_normed_one = (
        product(grad_query_low, back_query)
        + product(grad_key_low, back_key)
        + product(grad_value_low, back_value)
    )
    gain_one_grad = jnp.sum(grad_normed_one * unit_one, axis=0)
    input_grad = grad_hidden + norm_back(scale_one, unit_one, grad_normed_one * gain_one)
    summed = (
        lax.psum(attention_shards[0].astype(jnp.bfloat16), "ctx").astype(jnp.float32),
        lax.psum(attention_shards[1].astype(jnp.bfloat16), "ctx").astype(jnp.float32),
        lax.psum(attention_shards[2].astype(jnp.bfloat16), "ctx").astype(jnp.float32),
        lax.psum(attention_shards[3].astype(jnp.bfloat16), "ctx").astype(jnp.float32),
        lax.psum(feedforward_shards[0].astype(jnp.bfloat16), "ctx").astype(jnp.float32),
        lax.psum(feedforward_shards[1].astype(jnp.bfloat16), "ctx").astype(jnp.float32),
        lax.psum(feedforward_shards[2].astype(jnp.bfloat16), "ctx").astype(jnp.float32),
    )
    gain_sums = lax.psum((gain_one_grad, gain_two_grad), ("fsdp", "ctx"))
    return (
        layer_output,
        input_grad,
        gain_sums[0],
        summed[0],
        summed[1],
        summed[2],
        summed[3],
        gain_sums[1],
        summed[4],
        summed[5],
        summed[6],
    )


def solution(mesh):
    in_specs = (
        P(("fsdp", "ctx"), None),
        P(("fsdp", "ctx")),
        P(("fsdp", "ctx"), None),
        P(),
        P("fsdp", None),
        P("fsdp", None),
        P("fsdp", None),
        P("fsdp", None),
        P(),
        P("fsdp", None),
        P("fsdp", None),
        P("fsdp", None),
    )
    out_specs = (
        P(("fsdp", "ctx"), None),
        P(("fsdp", "ctx"), None),
        P(),
        P("fsdp", None),
        P("fsdp", None),
        P("fsdp", None),
        P("fsdp", None),
        P(),
        P("fsdp", None),
        P("fsdp", None),
        P("fsdp", None),
    )
    return jax.shard_map(
        per_device, mesh=mesh, in_specs=in_specs, out_specs=out_specs, check_vma=False
    )
```

profile of v0, /device:TPU:0, one launch (start us, length us, event | category | flops | bytes accessed | tf_op | source)
XLA Modules:
  0.0 1605.2 jit_solution(15687253532271398078)
XLA Ops:
  10.6 25.8 %all-gather.12.cloned.1.call-done = bf16[768,1536]{1,0:T(8,128)(2,1)} async-done(((bf16[192,1536]{1,0:T(8,128)(2,1)}), bf16[768,1536]{1,0:T(8,128)(2,1)}) %all-gather.12.cloned.1.call-update) | async-done | bytes 2359312 | tf_op jit(solution)/shard_map/all_gather | solution.py:207
  40.6 21.4 %all-gather.14.cloned.1.call-done = bf16[768,1536]{1,0:T(8,128)(2,1)} async-done(((bf16[192,1536]{1,0:T(8,128)(2,1)}), bf16[768,1536]{1,0:T(8,128)(2,1)}) %all-gather.14.cloned.1.call-update) | async-done | bytes 2359312 | tf_op jit(solution)/shard_map/all_gather | solution.py:206
  68.2 20.5 %all-gather.1 = s32[8,1,128]{2,1,0:T(1,128)S(1)} all-gather(s32[1,1,128]{2,1,0:T(1,128)S(1)} %bitcast.402), channel_id=1, replica_groups=mesh['fsdp'=4,'ctx'=8] {'ctx'}, dimensions={0}, use_global_device_ids=true | all-gather | bytes 4608 | tf_op jit(solution)/shard_map/all_gather | solution.py:219
  88.8 20.2 %all-gather.28.cloned.1.call-done = bf16[1024,768]{1,0:T(8,128)(2,1)} async-done(((bf16[128,768]{1,0:T(8,128)(2,1)}), bf16[1024,768]{1,0:T(8,128)(2,1)}) %all-gather.28.cloned.1.call-update) | async-done | bytes 1572880 | tf_op jit(solution)/shard_map/all_gather | solution.py:239
  110.7 35.5 %all-gather.18.cloned.1.call-done = bf16[1536,1536]{1,0:T(8,128)(2,1)} async-done(((bf16[384,1536]{1,0:T(8,128)(2,1)}), bf16[1536,1536]{1,0:T(8,128)(2,1)}) %all-gather.18.cloned.1.call-update) | async-done | bytes 4718608 | tf_op jit(solution)/shard_map/all_gather | solution.py:205
  150.2 43.0 %all-gather.16.cloned.1.call-done = bf16[1,1024,768]{1,2,0:T(8,128)(2,1)} async-done(((bf16[1,128,768]{1,2,0:T(8,128)(2,1)}), bf16[1,1024,768]{1,2,0:T(8,128)(2,1)}) %all-gather.16.cloned.1.call-update) | async-done | bytes 1572880 | tf_op jit(solution)/shard_map/all_gather | solution.py:238
  193.1 14.8 while.62
  218.6 11.6 all-gather.20.cloned.1.call-done
  233.6 80.3 %all-gather.22.cloned.1.call-done = bf16[4096,1536]{1,0:T(8,128)(2,1)} async-done(((bf16[1024,1536]{1,0:T(8,128)(2,1)}), bf16[4096,1536]{1,0:T(8,128)(2,1)}) %all-gather.22.cloned.1.call-update) | async-done | bytes 12582928 | tf_op jit(solution)/shard_map/all_gather | solution.py:213
  323.8 73.7 %all-gather.24.cloned.1.call-done = bf16[4096,1536]{1,0:T(8,128)(2,1)} async-done(((bf16[1024,1536]{1,0:T(8,128)(2,1)}), bf16[4096,1536]{1,0:T(8,128)(2,1)}) %all-gather.24.cloned.1.call-update) | async-done | bytes 12582928 | tf_op jit(solution)/shard_map/all_gather | solution.py:214
  397.5 10.0 fusion.112
  407.5 73.7 %all-gather.26.cloned.1.call-done = bf16[4096,1536]{1,0:T(8,128)(2,1)} async-done(((bf16[1024,1536]{1,0:T(8,128)(2,1)}), bf16[4096,1536]{1,0:T(8,128)(2,1)}) %all-gather.26.cloned.1.call-update) | async-done | bytes 12582928 | tf_op jit(solution)/shard_map/all_gather | solution.py:215
  481.2 11.2 multiply_convert_fusion
  518.7 25.2 %while.65 = (s32[]{:T(128)}, f32[1,128,8,2,96]{1,4,3,2,0:T(8,128)}, bf16[1,1024,8,96]{1,3,2,0:T(8,128)(2,1)}, bf16[1,1024,8,96]{1,3,2,0:T(8,128)(2,1)}, bf16[1,1...) while((s32[]{:T(128)}, f32[1,128,8,2,96]{1,4,3,2,0:T(8,128)}, ...), condition=%wide.region_13.14_spmd.clone, body=%wide.region_12.13_spmd.clone.sunk | while | flops 1018167296 | bytes 70744944 | solution.py:180
  564.6 56.8 %reduce-scatter.28.cloned.1.call-done = bf16[128,768]{1,0:T(8,128)(2,1)} async-done(((bf16[1024,768]{1,0:T(8,128)(2,1)}), bf16[128,768]{1,0:T(8,128)(2,1)}) %reduce-scatter.28.cloned.1.call-update) | async-done | bytes 196624
  625.5 64.5 %reduce-scatter.30.cloned.1.call-done = bf16[128,768]{1,0:T(8,128)(2,1)} async-done(((bf16[1024,768]{1,0:T(8,128)(2,1)}), bf16[128,768]{1,0:T(8,128)(2,1)}) %reduce-scatter.30.cloned.1.call-update) | async-done | bytes 196624
  725.9 34.6 %reduce-scatter.18.cloned.1.call-done = bf16[192,1536]{1,0:T(8,128)(2,1)} async-done(((bf16[768,1536]{1,0:T(8,128)(2,1)}), bf16[192,1536]{1,0:T(8,128)(2,1)}) %reduce-scatter.18.cloned.1.call-update) | async-done | bytes 589840 | tf_op jit(solution)/shard_map/reduce_scatter | solution.py:329
  760.5 51.0 %reduce-scatter.14.cloned.1.call-done = bf16[384,1536]{1,0:T(8,128)(2,1)} async-done(((bf16[1536,1536]{1,0:T(8,128)(2,1)}), bf16[384,1536]{1,0:T(8,128)(2,1)}) %reduce-scatter.14.cloned.1.call-update) | async-done | bytes 1179664 | tf_op jit(solution)/shard_map/reduce_scatter | solution.py:323
  811.5 51.0 %reduce-scatter.20.cloned.1.call-done = bf16[384,1536]{1,0:T(8,128)(2,1)} async-done(((bf16[1536,1536]{1,0:T(8,128)(2,1)}), bf16[384,1536]{1,0:T(8,128)(2,1)}) %reduce-scatter.20.cloned.1.call-update) | async-done | bytes 1179664 | tf_op jit(solution)/shard_map/reduce_scatter | solution.py:332
  862.4 102.1 %reduce-scatter.22.cloned.1.call-done = bf16[1024,1536]{1,0:T(8,128)(2,1)} async-done(((bf16[4096,1536]{1,0:T(8,128)(2,1)}), bf16[1024,1536]{1,0:T(8,128)(2,1)}) %reduce-scatter.22.cloned.1.call-update) | async-done | bytes 3145744 | tf_op jit(solution)/shard_map/reduce_scatter | solution.py:273
  964.5 102.1 %reduce-scatter.24.cloned.1.call-done = bf16[1024,1536]{1,0:T(8,128)(2,1)} async-done(((bf16[4096,1536]{1,0:T(8,128)(2,1)}), bf16[1024,1536]{1,0:T(8,128)(2,1)}) %reduce-scatter.24.cloned.1.call-update) | async-done | bytes 3145744 | tf_op jit(solution)/shard_map/reduce_scatter | solution.py:276
  1066.6 102.1 %reduce-scatter.26.cloned.1.call-done = bf16[1024,1536]{1,0:T(8,128)(2,1)} async-done(((bf16[4096,1536]{1,0:T(8,128)(2,1)}), bf16[1024,1536]{1,0:T(8,128)(2,1)}) %reduce-scatter.26.cloned.1.call-update) | async-done | bytes 3145744 | tf_op jit(solution)/shard_map/reduce_scatter | solution.py:279
  1182.4 44.1 %all-reduce = (f32[1536]{0:T(1024)}, f32[1536]{0:T(1024)}) all-reduce(f32[1536]{0:T(1024)S(1)} %get-tuple-element.788, f32[1536]{0:T(1024)S(1)} %get-tuple-element.786), channel_id=1, replica_groups=mesh['fsdp'=4,'ctx'=8] {'fsdp','ctx'}, use_global_device_ids=true, to_apply=%region_18.19 | all-reduce | flops 3072 | bytes 24576 | tf_op jit(solution)/shard_map/psum | solution.py:352
  1227.7 352.3 %all-reduce.4.cloned.1.call-done = (bf16[384,1536]{1,0:T(8,128)(2,1)}, bf16[192,1536]{1,0:T(8,128)(2,1)}, bf16[192,1536]{1,0:T(8,128)(2,1)}, bf16[384,1536]{1,0:...) async-done(((bf16[384,1536]{1,0:T(8,128)(2,1)}, bf16[192,1536]{1,0:T(8,128)(2,1)}, bf16[192,1536]{1,0:T(8,128)(2,1)}, ...) | async-done | bytes 12976144 | tf_op jit(solution)/shard_map/psum | solution.py:344
  (239 shorter events, 217.7 us)
Async XLA Ops:
  7.2 54.8 %copy-start.2 = (bf16[128,1536]{1,0:T(8,128)(2,1)S(1)}, bf16[128,1536]{1,0:T(8,128)(2,1)}, u32[]{:S(2)}) copy-start(bf16[128,1536]{1,0:T(8,128)(2,1)} %param.20) | copy-start | bytes 1179652
  7.2 33.2 %copy-start.33 = (s32[128]{0:T(128)S(1)}, s32[128]{0:T(128)}, u32[]{:S(2)}) copy-start(s32[128]{0:T(128)} %param.21) | copy-start | bytes 1540
  7.2 29.2 %all-gather.12.cloned.1.call-start = ((), (), s32[]{:S(2)}) async-start(), calls=%async_computation.9 | async-start | bytes 2949120 | tf_op jit(solution)/shard_map/all_gather | solution.py:207
  7.9 54.1 %all-gather.14.cloned.1.call-start = ((), (), s32[]{:S(2)}) async-start(), calls=%async_computation.10 | async-start | bytes 2949120 | tf_op jit(solution)/shard_map/all_gather | solution.py:206
  8.7 100.3 %all-gather.28.cloned.1.call-start = ((), (), s32[]{:S(2)}) async-start(), calls=%async_computation.24 | async-start | bytes 1769472 | tf_op jit(solution)/shard_map/all_gather | solution.py:239
  39.8 106.5 %all-gather.18.cloned.1.call-start = ((), (), s32[]{:S(2)}) async-start(), calls=%async_computation.12 | async-start | bytes 5898240 | tf_op jit(solution)/shard_map/all_gather | solution.py:205
  40.4 152.8 %all-gather.16.cloned.1.call-start = ((), (), s32[]{:S(2)}) async-start(), calls=%async_computation.11 | async-start | bytes 1769472 | tf_op jit(solution)/shard_map/all_gather | solution.py:238
  65.3 164.9 %all-gather.20.cloned.1.call-start = ((), (), s32[]{:S(2)}) async-start(), calls=%async_computation.13 | async-start | bytes 5898240 | tf_op jit(solution)/shard_map/all_gather | solution.py:208
  65.9 248.0 %all-gather.22.cloned.1.call-start = ((), (), s32[]{:S(2)}) async-start(), calls=%async_computation.14 | async-start | bytes 15728640 | tf_op jit(solution)/shard_map/all_gather | solution.py:213
  66.6 330.9 %all-gather.24.cloned.1.call-start = ((), (), s32[]{:S(2)}) async-start(), calls=%async_computation.15 | async-start | bytes 15728640 | tf_op jit(solution)/shard_map/all_gather | solution.py:214
  67.4 413.8 %all-gather.26.cloned.1.call-start = ((), (), s32[]{:S(2)}) async-start(), calls=%async_computation.16 | async-start | bytes 15728640 | tf_op jit(solution)/shard_map/all_gather | solution.py:215
  68.1 553.3 %reduce-scatter.28.cloned.1.call-start = ((), (), s32[]{:S(2)}) async-start(), calls=%async_computation.25 | async-start | bytes 1769472
  218.6 105.3 %copy-start.16 = (bf16[1,128,8,2,96]{1,4,3,2,0:T(8,128)(2,1)}, bf16[1,128,8,2,96]{1,4,3,2,0:T(8,128)(2,1)S(1)}, u32[]{:S(2)}) copy-start(bf16[1,128,8,2,96]{1,4,3,2,0:T(8,128)(2,1)S(1)} %convert_element_type.192) | copy-start | bytes 1179652
  233.4 272.9 %copy-start.4 = (f32[128,1536]{1,0:T(8,128)}, f32[128,1536]{1,0:T(8,128)S(1)}, u32[]{:S(2)}) copy-start(f32[128,1536]{1,0:T(8,128)S(1)} %get-tuple-element.887) | copy-start | bytes 2359300
  555.6 134.4 %reduce-scatter.30.cloned.1.call-start = ((), (), s32[]{:S(2)}) async-start(), calls=%async_computation.26 | async-start | bytes 1769472
  564.6 161.4 %reduce-scatter.16.cloned.1.call-start = ((), (), s32[]{:S(2)}) async-start(), calls=%async_computation.18 | async-start | bytes 2949120 | tf_op jit(solution)/shard_map/reduce_scatter | solution.py:326
  625.4 68.5 %copy-start.3 = (f32[1,128,8,2,96]{1,4,3,2,0:T(8,128)S(1)}, f32[1,128,8,2,96]{1,4,3,2,0:T(8,128)}, u32[]{:S(2)}) copy-start(f32[1,128,8,2,96]{1,4,3,2,0:T(8,128)} %get-tuple-element.634) | copy-start | bytes 2359300
  625.4 135.1 %reduce-scatter.18.cloned.1.call-start = ((), (), s32[]{:S(2)}) async-start(), calls=%async_computation.19 | async-start | bytes 2949120 | tf_op jit(solution)/shard_map/reduce_scatter | solution.py:329
  693.9 117.6 %reduce-scatter.14.cloned.1.call-start = ((), (), s32[]{:S(2)}) async-start(), calls=%async_computation.17 | async-start | bytes 5898240 | tf_op jit(solution)/shard_map/reduce_scatter | solution.py:323
  697.8 164.7 %reduce-scatter.20.cloned.1.call-start = ((), (), s32[]{:S(2)}) async-start(), calls=%async_computation.20 | async-start | bytes 5898240 | tf_op jit(solution)/shard_map/reduce_scatter | solution.py:332
  702.7 261.9 %reduce-scatter.22.cloned.1.call-start = ((), (), s32[]{:S(2)}) async-start(), calls=%async_computation.21 | async-start | bytes 15728640 | tf_op jit(solution)/shard_map/reduce_scatter | solution.py:273
  710.5 356.2 %reduce-scatter.24.cloned.1.call-start = ((), (), s32[]{:S(2)}) async-start(), calls=%async_computation.22 | async-start | bytes 15728640 | tf_op jit(solution)/shard_map/reduce_scatter | solution.py:276
  718.1 450.6 %reduce-scatter.26.cloned.1.call-start = ((), (), s32[]{:S(2)}) async-start(), calls=%async_computation.23 | async-start | bytes 15728640 | tf_op jit(solution)/shard_map/reduce_scatter | solution.py:279
  725.9 854.1 %all-reduce.4.cloned.1.call-start = ((), (), s32[]{:S(2)}) async-start(), calls=%async_computation.27 | async-start | bytes 25952256 | tf_op jit(solution)/shard_map/psum | solution.py:344
  (38 other events, 133.9 us)
Sparse Core Ops, SparseCore 0:
  9.6 26.7 all-gather.11
  37.9 24.0 all-gather.13
  64.8 44.1 all-gather.27
  110.4 35.7 all-gather.17
  148.7 44.4 all-gather.15
  194.6 35.5 all-gather.19
  231.8 82.0 all-gather.21
  315.4 82.0 all-gather.23
  399.1 82.0 all-gather.25
  555.7 65.6 reduce-scatter.27
  625.4 64.5 reduce-scatter.29
  693.0 31.5 reduce-scatter.15
  727.7 32.8 reduce-scatter.17
  763.5 47.9 reduce-scatter.13
  814.4 47.9 reduce-scatter.19
  864.9 99.6 reduce-scatter.21
  967.0 99.6 reduce-scatter.23
  1069.1 99.6 reduce-scatter.25
  1174.4 405.4 all-reduce.3
where the time goes:
time: 1610 us
  waiting for transfers between devices  1310 us (81%)
  matrix products  149 us (9%)
  blocking collectives  64.7 us (4%)
  local copies, waits for them, and re-layouts  36.1 us (2%)
  other arithmetic  32 us (2%)
    psum x1, waiting for transfers between devices, per_device(): lax.psum(attention_shards[0].astype(jnp.bfloat16), 'ctx')  352 us
    unnamed x21, waiting for transfers between devices  126 us
    reduce_scatter x1, waiting for transfers between devices, per_device(): lax.psum_scatter(grad_gate.astype(jnp.bfloat16), 'fsdp', scatter_dimensio...  102 us
    reduce_scatter x1, waiting for transfers between devices, per_device(): lax.psum_scatter(grad_down.astype(jnp.bfloat16), 'fsdp', scatter_dimensio...  102 us
    reduce_scatter x1, waiting for transfers between devices, per_device(): lax.psum_scatter(grad_up.astype(jnp.bfloat16), 'fsdp', scatter_dimension=...  102 us
    all_gather x1, waiting for transfers between devices, feedforward_set(): lax.all_gather(gate_weight, 'fsdp', axis=0, tiled=True)  80.3 us
    all_gather x1, waiting for transfers between devices, feedforward_set(): lax.all_gather(down_weight, 'fsdp', axis=0, tiled=True)  73.7 us
    all_gather x1, waiting for transfers between devices, feedforward_set(): lax.all_gather(up_weight, 'fsdp', axis=0, tiled=True)  73.7 us
  transfers between devices with their start and end apart: 19, of which 18 were waited for; matrix products, arithmetic and copies ran while one was open for 7% of the time, Pallas kernels for 0%

commit v1 on v0

--- a/solution.py
+++ b/solution.py
@@ -341,7 +341,9 @@
     gain_one_grad = jnp.sum(grad_normed_one * unit_one, axis=0)
     input_grad = grad_hidden + norm_back(scale_one, unit_one, grad_normed_one * gain_one)
     summed = (
-        lax.psum(attention_shards[0].astype(jnp.bfloat16), "ctx").astype(jnp.float32),
+        jnp.sum(lax.all_gather(attention_shards[0].astype(jnp.bfloat16), "ctx"), axis=0).astype(
+            jnp.float32
+        ),
         lax.psum(attention_shards[1].astype(jnp.bfloat16), "ctx").astype(jnp.float32),
         lax.psum(attention_shards[2].astype(jnp.bfloat16), "ctx").astype(jnp.float32),
         lax.psum(attention_shards[3].astype(jnp.bfloat16), "ctx").astype(jnp.float32),

time: 1610 us -> 1710 us (1.062)
  waiting for transfers between devices: 1310 us -> 1390 us
    all_gather x0 -> x1, waiting for transfers between devices: none -> 81.9 us  [per_device(): lax.all_gather(attention_shards[0].astype(jnp.bfloat16), 'ctx')]
    reduce_scatter x1, waiting for transfers between devices: 0.02 us -> 35.9 us  [per_device(): lax.psum_scatter(grad_key.astype(jnp.bfloat16), 'fsdp', scatter_dimension...]
    reduce_scatter x1, waiting for transfers between devices: 51 us -> 18.5 us  [per_device(): lax.psum_scatter(grad_query.astype(jnp.bfloat16), 'fsdp', scatter_dimensi...]
    unnamed x21 -> x22, waiting for transfers between devices: 126 us -> 122 us
  transfers between devices with their start and end apart: 19 -> 20, of which waited for: 18 -> 20; matrix products, arithmetic and copies ran while one was open for 7% -> 7% of each run, Pallas kernels for 0% -> 0%
where the time goes in v1:
time: 1710 us; the launch traced here: 1700 us
  waiting for transfers between devices  1390 us (81%)
  matrix products  150 us (9%)
  blocking collectives  64.9 us (4%)
  other arithmetic  37.7 us (2%)
  local copies, waits for them, and re-layouts  34.6 us (2%)
    psum x1, waiting for transfers between devices, per_device(): lax.psum(attention_shards[1].astype(jnp.bfloat16), 'ctx')  358 us
    unnamed x22, waiting for transfers between devices  122 us
    reduce_scatter x1, waiting for transfers between devices, per_device(): lax.psum_scatter(grad_down.astype(jnp.bfloat16), 'fsdp', scatter_dimensio...  102 us
    reduce_scatter x1, waiting for transfers between devices, per_device(): lax.psum_scatter(grad_gate.astype(jnp.bfloat16), 'fsdp', scatter_dimensio...  102 us
    reduce_scatter x1, waiting for transfers between devices, per_device(): lax.psum_scatter(grad_up.astype(jnp.bfloat16), 'fsdp', scatter_dimension=...  102 us
    all_gather x1, waiting for transfers between devices, per_device(): lax.all_gather(attention_shards[0].astype(jnp.bfloat16), 'ctx')  81.9 us
    all_gather x1, waiting for transfers between devices, feedforward_set(): lax.all_gather(gate_weight, 'fsdp', axis=0, tiled=True)  80.3 us
    all_gather x1, waiting for transfers between devices, feedforward_set(): lax.all_gather(down_weight, 'fsdp', axis=0, tiled=True)  73.7 us
  transfers between devices with their start and end apart: 20, of which 20 were waited for; matrix products, arithmetic and copies ran while one was open for 7% of the time, Pallas kernels for 0%

profile of v1, /device:TPU:0, one launch (start us, length us, event | category | flops | bytes accessed | tf_op | source)
XLA Modules:
  0.0 1698.9 jit_solution(11883376395268189844)
XLA Ops:
  10.6 25.8 %all-gather.14.cloned.1.call-done = bf16[768,1536]{1,0:T(8,128)(2,1)} async-done(((bf16[192,1536]{1,0:T(8,128)(2,1)}), bf16[768,1536]{1,0:T(8,128)(2,1)}) %all-gather.14.cloned.1.call-update) | async-done | bytes 2359312 | tf_op jit(solution)/shard_map/all_gather | solution.py:207
  40.6 21.4 %all-gather.16.cloned.1.call-done = bf16[768,1536]{1,0:T(8,128)(2,1)} async-done(((bf16[192,1536]{1,0:T(8,128)(2,1)}), bf16[768,1536]{1,0:T(8,128)(2,1)}) %all-gather.16.cloned.1.call-update) | async-done | bytes 2359312 | tf_op jit(solution)/shard_map/all_gather | solution.py:206
  68.2 20.5 %all-gather.2 = s32[8,1,128]{2,1,0:T(1,128)S(1)} all-gather(s32[1,1,128]{2,1,0:T(1,128)S(1)} %bitcast.404), channel_id=1, replica_groups=mesh['fsdp'=4,'ctx'=8] {'ctx'}, dimensions={0}, use_global_device_ids=true | all-gather | bytes 4608 | tf_op jit(solution)/shard_map/all_gather | solution.py:219
  88.8 20.2 %all-gather.30.cloned.1.call-done = bf16[1024,768]{1,0:T(8,128)(2,1)} async-done(((bf16[128,768]{1,0:T(8,128)(2,1)}), bf16[1024,768]{1,0:T(8,128)(2,1)}) %all-gather.30.cloned.1.call-update) | async-done | bytes 1572880 | tf_op jit(solution)/shard_map/all_gather | solution.py:239
  110.7 35.5 %all-gather.20.cloned.1.call-done = bf16[1536,1536]{1,0:T(8,128)(2,1)} async-done(((bf16[384,1536]{1,0:T(8,128)(2,1)}), bf16[1536,1536]{1,0:T(8,128)(2,1)}) %all-gather.20.cloned.1.call-update) | async-done | bytes 4718608 | tf_op jit(solution)/shard_map/all_gather | solution.py:205
  150.2 43.0 %all-gather.18.cloned.1.call-done = bf16[1,1024,768]{1,2,0:T(8,128)(2,1)} async-done(((bf16[1,128,768]{1,2,0:T(8,128)(2,1)}), bf16[1,1024,768]{1,2,0:T(8,128)(2,1)}) %all-gather.18.cloned.1.call-update) | async-done | bytes 1572880 | tf_op jit(solution)/shard_map/all_gather | solution.py:238
  193.1 14.8 while.62
  218.6 11.6 all-gather.22.cloned.1.call-done
  233.6 80.3 %all-gather.24.cloned.1.call-done = bf16[4096,1536]{1,0:T(8,128)(2,1)} async-done(((bf16[1024,1536]{1,0:T(8,128)(2,1)}), bf16[4096,1536]{1,0:T(8,128)(2,1)}) %all-gather.24.cloned.1.call-update) | async-done | bytes 12582928 | tf_op jit(solution)/shard_map/all_gather | solution.py:213
  323.8 73.7 %all-gather.26.cloned.1.call-done = bf16[4096,1536]{1,0:T(8,128)(2,1)} async-done(((bf16[1024,1536]{1,0:T(8,128)(2,1)}), bf16[4096,1536]{1,0:T(8,128)(2,1)}) %all-gather.26.cloned.1.call-update) | async-done | bytes 12582928 | tf_op jit(solution)/shard_map/all_gather | solution.py:214
  407.5 73.7 %all-gather.28.cloned.1.call-done = bf16[4096,1536]{1,0:T(8,128)(2,1)} async-done(((bf16[1024,1536]{1,0:T(8,128)(2,1)}), bf16[4096,1536]{1,0:T(8,128)(2,1)}) %all-gather.28.cloned.1.call-update) | async-done | bytes 12582928 | tf_op jit(solution)/shard_map/all_gather | solution.py:215
  518.7 25.2 %while.65 = (s32[]{:T(128)}, f32[1,128,8,2,96]{1,4,3,2,0:T(8,128)}, bf16[1,1024,8,96]{1,3,2,0:T(8,128)(2,1)}, bf16[1,1024,8,96]{1,3,2,0:T(8,128)(2,1)}, bf16[1,1...) while((s32[]{:T(128)}, f32[1,128,8,2,96]{1,4,3,2,0:T(8,128)}, ...), condition=%wide.region_13.14_spmd.clone, body=%wide.region_12.13_spmd.clone.sunk | while | flops 1018167296 | bytes 70744944 | solution.py:180
  568.7 52.8 %reduce-scatter.28.cloned.1.call-done = bf16[128,768]{1,0:T(8,128)(2,1)} async-done(((bf16[1024,768]{1,0:T(8,128)(2,1)}), bf16[128,768]{1,0:T(8,128)(2,1)}) %reduce-scatter.28.cloned.1.call-update) | async-done | bytes 196624
  625.5 64.5 %reduce-scatter.30.cloned.1.call-done = bf16[128,768]{1,0:T(8,128)(2,1)} async-done(((bf16[1024,768]{1,0:T(8,128)(2,1)}), bf16[128,768]{1,0:T(8,128)(2,1)}) %reduce-scatter.30.cloned.1.call-update) | async-done | bytes 196624
  721.3 18.5 %reduce-scatter.14.cloned.1.call-done = bf16[384,1536]{1,0:T(8,128)(2,1)} async-done(((bf16[1536,1536]{1,0:T(8,128)(2,1)}), bf16[384,1536]{1,0:T(8,128)(2,1)}) %reduce-scatter.14.cloned.1.call-update) | async-done | bytes 1179664 | tf_op jit(solution)/shard_map/reduce_scatter | solution.py:323
  739.9 35.9 %reduce-scatter.16.cloned.1.call-done = bf16[192,1536]{1,0:T(8,128)(2,1)} async-done(((bf16[768,1536]{1,0:T(8,128)(2,1)}), bf16[192,1536]{1,0:T(8,128)(2,1)}) %reduce-scatter.16.cloned.1.call-update) | async-done | bytes 589840 | tf_op jit(solution)/shard_map/reduce_scatter | solution.py:326
  775.7 35.8 %reduce-scatter.18.cloned.1.call-done = bf16[192,1536]{1,0:T(8,128)(2,1)} async-done(((bf16[768,1536]{1,0:T(8,128)(2,1)}), bf16[192,1536]{1,0:T(8,128)(2,1)}) %reduce-scatter.18.cloned.1.call-update) | async-done | bytes 589840 | tf_op jit(solution)/shard_map/reduce_scatter | solution.py:329
  811.6 51.0 %reduce-scatter.20.cloned.1.call-done = bf16[384,1536]{1,0:T(8,128)(2,1)} async-done(((bf16[1536,1536]{1,0:T(8,128)(2,1)}), bf16[384,1536]{1,0:T(8,128)(2,1)}) %reduce-scatter.20.cloned.1.call-update) | async-done | bytes 1179664 | tf_op jit(solution)/shard_map/reduce_scatter | solution.py:332
  862.5 102.1 %reduce-scatter.22.cloned.1.call-done = bf16[1024,1536]{1,0:T(8,128)(2,1)} async-done(((bf16[4096,1536]{1,0:T(8,128)(2,1)}), bf16[1024,1536]{1,0:T(8,128)(2,1)}) %reduce-scatter.22.cloned.1.call-update) | async-done | bytes 3145744 | tf_op jit(solution)/shard_map/reduce_scatter | solution.py:273
  964.6 102.1 %reduce-scatter.24.cloned.1.call-done = bf16[1024,1536]{1,0:T(8,128)(2,1)} async-done(((bf16[4096,1536]{1,0:T(8,128)(2,1)}), bf16[1024,1536]{1,0:T(8,128)(2,1)}) %reduce-scatter.24.cloned.1.call-update) | async-done | bytes 3145744 | tf_op jit(solution)/shard_map/reduce_scatter | solution.py:276
  1066.7 102.1 %reduce-scatter.26.cloned.1.call-done = bf16[1024,1536]{1,0:T(8,128)(2,1)} async-done(((bf16[4096,1536]{1,0:T(8,128)(2,1)}), bf16[1024,1536]{1,0:T(8,128)(2,1)}) %reduce-scatter.26.cloned.1.call-update) | async-done | bytes 3145744 | tf_op jit(solution)/shard_map/reduce_scatter | solution.py:279
  1181.9 44.3 %all-reduce = (f32[1536]{0:T(1024)}, f32[1536]{0:T(1024)}) all-reduce(f32[1536]{0:T(1024)S(1)} %get-tuple-element.788, f32[1536]{0:T(1024)S(1)} %get-tuple-element.786), channel_id=1, replica_groups=mesh['fsdp'=4,'ctx'=8] {'fsdp','ctx'}, use_global_device_ids=true, to_apply=%region_18.19 | all-reduce | flops 3072 | bytes 24576 | tf_op jit(solution)/shard_map/psum | solution.py:354
  1227.4 81.9 %all-gather.32.cloned.1.call-done = bf16[3072,1536]{1,0:T(8,128)(2,1)} async-done(((bf16[384,1536]{1,0:T(8,128)(2,1)}), bf16[3072,1536]{1,0:T(8,128)(2,1)}) %all-gather.32.cloned.1.call-update) | async-done | bytes 9437200 | tf_op jit(solution)/shard_map/all_gather | solution.py:344
  1316.8 358.2 %all-reduce.4.cloned.1.call-done = (bf16[192,1536]{1,0:T(8,128)(2,1)}, bf16[192,1536]{1,0:T(8,128)(2,1)}, bf16[384,1536]{1,0:T(8,128)(2,1)}, bf16[1024,1536]{1,0...) async-done(((bf16[192,1536]{1,0:T(8,128)(2,1)}, bf16[192,1536]{1,0:T(8,128)(2,1)}, bf16[384,1536]{1,0:T(8,128)(2,1)}, bf16[1024,1536]{1,0:T(8,128)(2,1)}, ...) | async-done | bytes 11796496 | tf_op jit(solution)/shard_map/psum | solution.py:347
  (241 shorter events, 243.4 us)
Async XLA Ops:
  7.2 29.2 %all-gather.14.cloned.1.call-start = ((), (), s32[]{:S(2)}) async-start(), calls=%async_computation.9 | async-start | bytes 2949120 | tf_op jit(solution)/shard_map/all_gather | solution.py:207
  7.9 54.1 %all-gather.16.cloned.1.call-start = ((), (), s32[]{:S(2)}) async-start(), calls=%async_computation.10 | async-start | bytes 2949120 | tf_op jit(solution)/shard_map/all_gather | solution.py:206
  8.7 100.3 %all-gather.30.cloned.1.call-start = ((), (), s32[]{:S(2)}) async-start(), calls=%async_computation.24 | async-start | bytes 1769472 | tf_op jit(solution)/shard_map/all_gather | solution.py:239
  39.8 106.5 %all-gather.20.cloned.1.call-start = ((), (), s32[]{:S(2)}) async-start(), calls=%async_computation.12 | async-start | bytes 5898240 | tf_op jit(solution)/shard_map/all_gather | solution.py:205
  40.4 152.8 %all-gather.18.cloned.1.call-start = ((), (), s32[]{:S(2)}) async-start(), calls=%async_computation.11 | async-start | bytes 1769472 | tf_op jit(solution)/shard_map/all_gather | solution.py:238
  65.3 164.9 %all-gather.22.cloned.1.call-start = ((), (), s32[]{:S(2)}) async-start(), calls=%async_computation.13 | async-start | bytes 5898240 | tf_op jit(solution)/shard_map/all_gather | solution.py:208
  65.9 248.0 %all-gather.24.cloned.1.call-start = ((), (), s32[]{:S(2)}) async-start(), calls=%async_computation.14 | async-start | bytes 15728640 | tf_op jit(solution)/shard_map/all_gather | solution.py:213
  66.6 330.9 %all-gather.26.cloned.1.call-start = ((), (), s32[]{:S(2)}) async-start(), calls=%async_computation.15 | async-start | bytes 15728640 | tf_op jit(solution)/shard_map/all_gather | solution.py:214
  67.4 413.8 %all-gather.28.cloned.1.call-start = ((), (), s32[]{:S(2)}) async-start(), calls=%async_computation.16 | async-start | bytes 15728640 | tf_op jit(solution)/shard_map/all_gather | solution.py:215
  68.1 553.4 %reduce-scatter.28.cloned.1.call-start = ((), (), s32[]{:S(2)}) async-start(), calls=%async_computation.26 | async-start | bytes 1769472
  218.6 105.3 %copy-start.16 = (bf16[1,128,8,2,96]{1,4,3,2,0:T(8,128)(2,1)}, bf16[1,128,8,2,96]{1,4,3,2,0:T(8,128)(2,1)S(1)}, u32[]{:S(2)}) copy-start(bf16[1,128,8,2,96]{1,4,3,2,0:T(8,128)(2,1)S(1)} %convert_element_type.194) | copy-start | bytes 1179652
  233.4 272.9 %copy-start.4 = (f32[128,1536]{1,0:T(8,128)}, f32[128,1536]{1,0:T(8,128)S(1)}, u32[]{:S(2)}) copy-start(f32[128,1536]{1,0:T(8,128)S(1)} %get-tuple-element.886) | copy-start | bytes 2359300
  555.7 134.4 %reduce-scatter.30.cloned.1.call-start = ((), (), s32[]{:S(2)}) async-start(), calls=%async_computation.27 | async-start | bytes 1769472
  564.7 175.1 %reduce-scatter.14.cloned.1.call-start = ((), (), s32[]{:S(2)}) async-start(), calls=%async_computation.17 | async-start | bytes 5898240 | tf_op jit(solution)/shard_map/reduce_scatter | solution.py:323
  568.6 207.1 %reduce-scatter.16.cloned.1.call-start = ((), (), s32[]{:S(2)}) async-start(), calls=%async_computation.18 | async-start | bytes 2949120 | tf_op jit(solution)/shard_map/reduce_scatter | solution.py:326
  625.4 68.7 %copy-start.7 = (f32[128,1536]{1,0:T(8,128)S(1)}, f32[128,1536]{1,0:T(8,128)}, u32[]{:S(2)}) copy-start(f32[128,1536]{1,0:T(8,128)} %copy-done.6) | copy-start | bytes 2359300
  625.4 68.7 %copy-start.17 = (bf16[1,128,8,2,96]{1,4,3,2,0:T(8,128)(2,1)S(1)}, bf16[1,128,8,2,96]{1,4,3,2,0:T(8,128)(2,1)}, u32[]{:S(2)}) copy-start(bf16[1,128,8,2,96]{1,4,3,2,0:T(8,128)(2,1)} %copy-done.16) | copy-start | bytes 1179652
  625.5 186.1 %reduce-scatter.18.cloned.1.call-start = ((), (), s32[]{:S(2)}) async-start(), calls=%async_computation.19 | async-start | bytes 2949120 | tf_op jit(solution)/shard_map/reduce_scatter | solution.py:329
  693.9 168.6 %reduce-scatter.20.cloned.1.call-start = ((), (), s32[]{:S(2)}) async-start(), calls=%async_computation.20 | async-start | bytes 5898240 | tf_op jit(solution)/shard_map/reduce_scatter | solution.py:332
  697.9 266.7 %reduce-scatter.22.cloned.1.call-start = ((), (), s32[]{:S(2)}) async-start(), calls=%async_computation.21 | async-start | bytes 15728640 | tf_op jit(solution)/shard_map/reduce_scatter | solution.py:273
  705.7 361.0 %reduce-scatter.24.cloned.1.call-start = ((), (), s32[]{:S(2)}) async-start(), calls=%async_computation.22 | async-start | bytes 15728640 | tf_op jit(solution)/shard_map/reduce_scatter | solution.py:276
  713.5 455.3 %reduce-scatter.26.cloned.1.call-start = ((), (), s32[]{:S(2)}) async-start(), calls=%async_computation.23 | async-start | bytes 15728640 | tf_op jit(solution)/shard_map/reduce_scatter | solution.py:279
  721.3 588.1 %all-gather.32.cloned.1.call-start = ((), (), s32[]{:S(2)}) async-start(), calls=%async_computation.25 | async-start | bytes 10616832 | tf_op jit(solution)/shard_map/all_gather | solution.py:344
  739.8 935.2 %all-reduce.4.cloned.1.call-start = ((), (), s32[]{:S(2)}) async-start(), calls=%async_computation.28 | async-start | bytes 23592960 | tf_op jit(solution)/shard_map/psum | solution.py:347
  (38 other events, 220.5 us)
Sparse Core Ops, SparseCore 0:
  9.6 26.7 all-gather.13
  37.9 24.0 all-gather.15
  64.8 44.1 all-gather.29
  110.4 35.7 all-gather.19
  148.7 44.4 all-gather.17
  194.6 35.5 all-gather.21
  231.8 82.0 all-gather.23
  315.4 82.0 all-gather.25
  399.1 82.0 all-gather.27
  555.8 65.6 reduce-scatter.27
  625.5 64.5 reduce-scatter.29
  693.0 46.7 reduce-scatter.13
  742.9 32.8 reduce-scatter.15
  778.7 32.8 reduce-scatter.17
  814.5 47.9 reduce-scatter.19
  865.0 99.6 reduce-scatter.21
  967.1 99.6 reduce-scatter.23
  1069.2 99.6 reduce-scatter.25
  1171.0 138.3 all-gather.31
  1314.4 360.4 all-reduce.3
